TPU v7x, 256 devices: a whole 4x4x8 slice. The times are simulated.
256 devices in a mesh: grow: 16 (over y_lo, x, core), gcol: 16 (over z, y_hi).
Axes of the slice: x: 4, y: 4 (y_hi: 2, y_lo: 2; y = y_hi * 2 + y_lo), z: 8, core: 2. Of those that a mesh axis runs over, the one named last changes fastest.
Arguments:
- eps_static: float32 [12288, 12288], P('grow', 'gcol'), may hold values from -1.8 to 1.8
- eps_imag: float32 [12288, 12288], P('grow', 'gcol'), may hold values from -1.8 to 1.8
- frequency_grid: float32 [3], replicated, may hold values from 0.1 to 2
- band_energy: float32 [32], replicated, may hold values from -2 to 2
- pair_elements: bfloat16 [32, 64, 12288], P('grow', None, 'gcol'), may hold values from -0.0546875 to 0.0546875
Outputs:
- sigma: float32 [3, 64], P(None, 'gcol')
All inputs are finite; a program needn't handle non-finite values.
Results may differ from a plain program's by a relative error of at most 0.0019.
Values may be sent and summed in bfloat16 or wider, within the bound.
A program may use at most 64 MiB of HBM per device.

v0:
```python
import jax
import jax.numpy as jnp
from jax import lax
from jax.sharding import Mesh
from jax.sharding import PartitionSpec as P

NE = 3
GROW = ("grow_0", "grow_1", "grow_2")
GCOL = ("gcol_0", "gcol_1")


def gathered_by_axis(shard, axes, dim):
    for axis in reversed(axes):
        shard = lax.all_gather(shard, axis, axis=dim, tiled=True)
    return shard


def split_up(shard, dim, devices):
    lengths = shard.shape
    parts = shard.reshape(*lengths[:dim], devices, lengths[dim] // devices, *lengths[dim + 1 :])
    return jnp.moveaxis(parts, dim, 0)


def joined_along(parts, dim):
    lengths = list(parts.shape[1:])
    lengths[dim] *= parts.shape[0]
    return jnp.moveaxis(parts, 0, dim).reshape(lengths)


def turned_blocks(parts, axes, order):
    inside = parts.shape[1:]
    out = parts.reshape(*(lax.axis_size(a) for a in axes), *inside)
    for k in order:
        out = lax.all_to_all(out, axes[k], k, k, tiled=True)
    return out.reshape(-1, *inside)


def core_and_chips(shard, groups, order, split_dim, concat_dim):
    devices = lax.axis_size(groups[0]) * lax.axis_size(groups[1])
    parts = split_up(shard, split_dim, devices)
    return joined_along(turned_blocks(parts, groups, order), concat_dim)


def summed_on_arrival(shard, axis, dim):
    devices = lax.axis_size(axis)
    parts = lax.all_to_all(split_up(shard, dim, devices), axis, 0, 0, tiled=True)
    return jnp.sum(parts, axis=0)


def from_everyone(shard, axis):
    copies = jnp.broadcast_to(shard, (lax.axis_size(axis), *shard.shape))
    return lax.all_to_all(copies, axis, split_axis=0, concat_axis=0, tiled=True)


def of_everyone(shard, axis):
    everything = from_everyone(shard, axis)
    return jnp.sum(everything, axis=0)


def shards(eps_static, eps_imag, frequency_grid, band_energy, pair_elements):
    row_count = lax.axis_size(GROW)
    row_index = lax.axis_index(GROW)
    col_index = lax.axis_index(GCOL)
    height = eps_static.shape[0]
    breadth = eps_static.shape[1]
    bands = pair_elements.shape[0] * row_count
    states = pair_elements.shape[1]
    column_panel = lax.all_gather(pair_elements, GROW, axis=0, tiled=True)
    own_bands = gathered_by_axis(pair_elements, GCOL, 2)
    row_panel = core_and_chips(own_bands, (("grow_0", "grow_1"), "grow_2"), (1, 0), 2, 0)
    global_rows = row_index * height + lax.iota(jnp.int32, height)
    global_cols = col_index * breadth + lax.iota(jnp.int32, breadth)
    kronecker = (global_rows[:, None] == global_cols[None, :]).astype(jnp.float32)
    static_part = eps_static - kronecker
    imag_part = eps_imag - kronecker
    spread = static_part - imag_part
    pole_square = (imag_part * imag_part + 0.25) / (spread * spread + 0.25)
    pole_freq = jnp.sqrt(pole_square)
    strength = -static_part * pole_square
    left_rows = row_panel.reshape(bands * states, height)
    right_rows = column_panel.reshape(bands * states, breadth)
    terms = []
    for point in range(NE):
        kernel = (strength / (pole_freq * (pole_freq + frequency_grid[point]))).astype(jnp.bfloat16)
        projected = jnp.dot(left_rows, kernel, preferred_element_type=jnp.float32)
        terms.append(jnp.sum(projected * right_rows, axis=1))
    quad = jnp.stack(terms).reshape(NE, bands, states)
    offset_energy = frequency_grid[:, None] - band_energy[None, :]
    weight = 1.0 / (1.0 + offset_energy * offset_energy)
    partial_sigma = jnp.einsum("em,ems->es", weight, quad)
    shares = summed_on_arrival(partial_sigma, GCOL, 1)
    return of_everyone(shares, GROW)


def solution(mesh):
    finer = Mesh(
        mesh.devices.reshape(2, 4, 2, 8, 2), ("grow_0", "grow_1", "grow_2", "gcol_0", "gcol_1")
    )
    in_specs = (P(GROW, GCOL), P(GROW, GCOL), P(), P(), P(GROW, None, GCOL))
    out_specs = P(None, GCOL)
    return jax.shard_map(
        shards, mesh=finer, in_specs=in_specs, out_specs=out_specs, check_vma=False
    )
```

profile of v0, /device:TPU:1, one launch (start us, length us, event | category | flops | bytes accessed | tf_op | source)
XLA Modules:
  0.0 211.0 jit_solution(8430354224616254626)
XLA Ops:
  6.5 0.0 all-gather.3.cloned.1.call-start
  6.5 10.5 %all_gather.9 = bf16[2,64,1536]{2,1,0:T(8,128)(2,1)} all-gather(bf16[2,64,768]{2,1,0:T(8,128)(2,1)} %param.9), channel_id=1, replica_groups=mesh['grow_0'=2,'grow_1'=4,'grow_2'=2,'gcol_0'=8,'gcol_1'=2] {'gcol_1'}, dimensions={2}, use_global_device_ids=true | all-gather | bytes 589824 | tf_op jit(solution)/shard_map/all_gather | solution.py:14
  17.0 0.0 all-gather.3.cloned.1.call-update
  17.0 0.0 all-gather.5.cloned.1.call-start
  17.1 0.7 all-gather.5.cloned.1.call-update
  17.8 46.2 %all-gather.3.cloned.1.call-done = bf16[2,64,12288]{2,1,0:T(8,128)(2,1)} async-done(((bf16[2,64,1536]{2,1,0:T(8,128)(2,1)}), bf16[2,64,12288]{2,1,0:T(8,128)(2,1)}) %all-gather.3.cloned.1.call-update) | async-done | bytes 3145744 | tf_op jit(solution)/shard_map/all_gather | solution.py:14
  64.0 2.7 %copy.47 = bf16[16,8,16,768]{3,2,1,0:T(8,128)(2,1)S(1)} copy(bf16[16,8,16,768]{3,1,2,0:T(8,128)(2,1)} %bitcast.42) | data formatting | bytes 6291456
  66.7 0.2 bitcast_bitcast_fusion
  66.9 1.0 copy.36
  67.9 0.3 copy.37
  68.3 7.1 %all_to_all.20 = bf16[8,2,2,64,768]{4,3,2,0,1:T(8,128)(2,1)S(1)} all-to-all(bf16[8,2,2,64,768]{4,3,2,0,1:T(8,128)(2,1)S(1)} %copy.37), channel_id=1, replica_groups=mesh['grow_0'=2,'grow_1'=4,'grow_2'=2,'gcol_0'=8,'gcol_1'=2] {'grow_2'}, dimensions={1} | all-to-all | bytes 6291456 | tf_op jit(solution)/shard_map/all_to_all | solution.py:34
  75.4 2.0 copy.38
  77.4 0.0 copy-start
  77.4 0.0 copy-start.1
  77.4 5.0 %all-to-all-start.1 = ((bf16[8,2,2,64,768]{4,3,2,1,0:T(8,128)(2,1)}), bf16[8,2,2,64,768]{4,3,2,1,0:T(8,128)(2,1)S(1)}, u32[]{:S(2)}, u32[]{:S(2)}) async-start(bf16[8,2,2,64,768]{4,3,2,1,0:T(8,128)(2,1)} %copy.38), calls=%async_computation.1 | async-start | bytes 6291456 | tf_op jit(solution)/shard_map/all_to_all | solution.py:34
  82.4 0.0 copy-done
  82.4 0.7 fusion.26
  83.1 0.0 copy-done.1
  83.1 0.1 divide_bitcast_fusion
  83.2 53.7 %all-gather.5.cloned.1.call-done = bf16[32,64,768]{2,1,0:T(8,128)(2,1)} async-done(((bf16[2,64,768]{2,1,0:T(8,128)(2,1)}), bf16[32,64,768]{2,1,0:T(8,128)(2,1)}) %all-gather.5.cloned.1.call-update) | async-done | bytes 3145744 | tf_op jit(solution)/shard_map/all_gather | solution.py:68
  136.8 5.0 %bitcast_convert_fusion = f32[2048,768]{1,0:T(8,128)} fusion(bf16[32,64,768]{2,1,0:T(8,128)(2,1)} %all-gather.5.cloned.1.call-done), kind=kLoop, calls=%fused_computation.12 | loop fusion | flops 1572864 | bytes 9437184 | tf_op jit(solution)/shard_map/convert_element_type | solution.py:86
  141.9 6.6 %copy.39 = f32[2048,768]{0,1:T(8,128)} copy(f32[2048,768]{1,0:T(8,128)} %bitcast_convert_fusion) | data formatting | bytes 12582912 | tf_op jit(solution)/shard_map/convert_element_type | solution.py:86
  148.5 0.0 all-to-all-done.1
  148.5 9.0 %fusion = bf16[2048]{0:T(1024)(128)(2,1)S(1)} fusion(f32[2048,768]{0,1:T(8,128)} %copy.39, bf16[2048,768]{1,0:T(8,128)(2,1)S(1)} %bitcast.39, f32[]{:T(128)} %bitcast.10, f32[768,768]{1,0:T(8,128)} %param.5, s32[768]{0:T(1024)S(1)} %get-tuple-element.8, s32[768]{0:T(1024)S(1)} %get-tuple-element.9, f32[768,768]{1,0:T(8,128)} %param.6), kind=kOutput, calls=%fused_computation.1 | convolution fusion | flops 2428499968 | bytes 14166020 | tf_op jit(solution)/shard_map/dot_general | solution.py:85
  157.5 0.1 stack.14
  157.6 9.0 %fusion.1 = bf16[2048]{0:T(1024)(128)(2,1)S(1)} fusion(f32[2048,768]{0,1:T(8,128)} %copy.39, bf16[2048,768]{1,0:T(8,128)(2,1)S(1)} %bitcast.40, f32[]{:T(128)} %bitcast.7, f32[768,768]{1,0:T(8,128)} %param.5, s32[768]{0:T(1024)S(1)} %get-tuple-element.8, s32[768]{0:T(1024)S(1)} %get-tuple-element.9, f32[768,768]{1,0:T(8,128)} %param.6), kind=kOutput, calls=%fused_computation.3 | convolution fusion | flops 2428499968 | bytes 14166020 | tf_op jit(solution)/shard_map/dot_general | solution.py:85
  166.6 0.1 stack.13
  166.7 9.0 %fusion.2 = bf16[2048]{0:T(1024)(128)(2,1)S(1)} fusion(f32[2048,768]{0,1:T(8,128)} %copy.39, bf16[2048,768]{1,0:T(8,128)(2,1)S(1)} %bitcast.41, f32[]{:T(128)} %bitcast.1, f32[768,768]{1,0:T(8,128)} %param.5, s32[768]{0:T(1024)S(1)} %get-tuple-element.8, s32[768]{0:T(1024)S(1)} %get-tuple-element.9, f32[768,768]{1,0:T(8,128)} %param.6), kind=kOutput, calls=%fused_computation.5 | convolution fusion | flops 2428499968 | bytes 14166020 | tf_op jit(solution)/shard_map/dot_general | solution.py:85
  175.7 0.1 stack.12
  175.8 0.1 fusion.18
  175.9 0.1 reshape.31
  176.0 17.6 %all_to_all.21 = f32[16,3,4]{2,1,0:T(4,128)S(1)} all-to-all(f32[16,3,4]{2,1,0:T(4,128)S(1)} %copy.42), channel_id=1, replica_groups=mesh['grow_0'=2,'grow_1'=4,'grow_2'=2,'gcol_0'=8,'gcol_1'=2] {'gcol_0','..., dimensions={0} | all-to-all | bytes 1536 | tf_op jit(solution)/shard_map/all_to_all | solution.py:46
  193.6 9.9 %all_to_all.22 = f32[16,3,4]{2,1,0:T(4,128)S(1)} all-to-all(f32[16,3,4]{2,1,0:T(4,128)S(1)} %broadcast_in_dim.2), channel_id=1, replica_groups=mesh['grow_0'=2,'grow_1'=4,'grow_2'=2,'gcol_0'=8,'gcol_1'=2] {'grow_0','..., dimensions={0} | all-to-all | bytes 1536 | tf_op jit(solution)/shard_map/all_to_all | solution.py:52
  203.5 0.6 reduce_sum.49
  (5 shorter events, 0.1 us)
Async XLA Ops:
  6.5 57.5 %all-gather.3.cloned.1.call-start = ((), (), s32[]{:S(2)}) async-start(), calls=%async_computation.4 | async-start | bytes 3538944 | tf_op jit(solution)/shard_map/all_gather | solution.py:14
  17.0 119.8 %all-gather.5.cloned.1.call-start = ((), (), s32[]{:S(2)}) async-start(), calls=%async_computation.5 | async-start | bytes 3342336 | tf_op jit(solution)/shard_map/all_gather | solution.py:68
  77.4 5.0 %copy-start = (f32[3]{0:T(128)S(1)}, f32[3]{0:T(128)}, u32[]{:S(2)}) copy-start(f32[3]{0:T(128)} %param.7) | copy-start | bytes 40
  77.4 5.7 %copy-start.1 = (f32[32]{0:T(128)S(1)}, f32[32]{0:T(128)}, u32[]{:S(2)}) copy-start(f32[32]{0:T(128)} %param.8) | copy-start | bytes 388
  77.4 71.1 %all-to-all-start.1 = ((bf16[8,2,2,64,768]{4,3,2,1,0:T(8,128)(2,1)}), bf16[8,2,2,64,768]{4,3,2,1,0:T(8,128)(2,1)S(1)}, u32[]{:S(2)}, u32[]{:S(2)}) async-start(bf16[8,2,2,64,768]{4,3,2,1,0:T(8,128)(2,1)} %copy.38), calls=%async_computation.1 | async-start | bytes 6291456 | tf_op jit(solution)/shard_map/all_to_all | solution.py:34
Sparse Core Ops, SparseCore 0:
  17.2 46.8 all-gather.2
  65.9 70.9 all-gather.4
where the time goes:
time: 211 us
  waiting for transfers between devices  101 us (48%)
  blocking collectives  45.1 us (21%)
  matrix products  27.1 us (13%)
  local copies, waits for them, and re-layouts  13.8 us (7%)
  between operations  13.5 us (6%)
  other arithmetic  5.74 us (3%)
  starting transfers between devices  5.07 us (2%)
    all_gather x1, waiting for transfers between devices, shards(): column_panel = lax.all_gather(pair_elements, GROW, axis=0, tiled=True)  53.7 us
    all_gather x1, waiting for transfers between devices, gathered_by_axis(): shard = lax.all_gather(shard, axis, axis=dim, tiled=True)  46.2 us
    dot_general x3, matrix products, shards(): projected = jnp.dot(left_rows, kernel, preferred_element_type=jnp.float32)  27 us
    all_to_all x1, blocking collectives, summed_on_arrival(): lax.all_to_all(split_up(shard, dim, devices), axis, 0, 0, tiled=True)  17.6 us
    all_gather x1, blocking collectives, gathered_by_axis(): shard = lax.all_gather(shard, axis, axis=dim, tiled=True)  10.5 us
    all_to_all x1, blocking collectives, from_everyone(): return lax.all_to_all(copies, axis, split_axis=0, concat_axis=0, tiled=True)  9.92 us
    all_to_all x1, blocking collectives, turned_blocks(): out = lax.all_to_all(out, axes[k], k, k, tiled=True)  7.13 us
    convert_element_type x1, local copies, waits for them, and re-layouts, shards(): terms.append(jnp.sum(projected * right_rows, axis=1))  6.6 us
  transfers between devices with their start and end apart: 3, of which 2 were waited for; matrix products, arithmetic and copies ran while one was open for 9% of the time, Pallas kernels for 0%

commit v1 on v0

--- a/solution.py
+++ b/solution.py
@@ -65,7 +65,9 @@
     breadth = eps_static.shape[1]
     bands = pair_elements.shape[0] * row_count
     states = pair_elements.shape[1]
-    column_panel = lax.all_gather(pair_elements, GROW, axis=0, tiled=True)
+    column_panel = jnp.concatenate(
+        lax.all_to_all(jnp.stack([pair_elements] * lax.axis_size(GROW)), GROW, 0, 0), axis=0
+    )
     own_bands = gathered_by_axis(pair_elements, GCOL, 2)
     row_panel = core_and_chips(own_bands, (("grow_0", "grow_1"), "grow_2"), (1, 0), 2, 0)
     global_rows = row_index * height + lax.iota(jnp.int32, height)

time: 211 us -> 237 us (1.12)
  waiting for transfers between devices: 101 us -> 113 us
  blocking collectives: 45.1 us -> 52.5 us
  starting transfers between devices: 5.07 us -> 9.21 us
    all_gather x1 -> x0, waiting for transfers between devices: 53.7 us -> none  [shards(): column_panel = lax.all_gather(pair_elements, GROW, axis=0, tiled=True)]
    all_to_all x0 -> x1, waiting for transfers between devices: none -> 40 us  [shards(): lax.all_to_all(jnp.stack([pair_elements] * lax.axis_size(GROW)), GROW, 0, 0)]
    all_to_all x1, waiting for transfers between devices: 0.01 us -> 25.9 us  [turned_blocks(): out = lax.all_to_all(out, axes[k], k, k, tiled=True)]
    all_to_all x1, blocking collectives: 9.92 us -> 19.4 us  [from_everyone(): return lax.all_to_all(copies, axis, split_axis=0, concat_axis=0, tiled=True)]
    all_to_all x0 -> x1, starting transfers between devices: none -> 5.56 us  [shards(): lax.all_to_all(jnp.stack([pair_elements] * lax.axis_size(GROW)), GROW, 0, 0)]
  transfers between devices with their start and end apart: 3 -> 3, of which waited for: 2 -> 3; matrix products, arithmetic and copies ran while one was open for 9% -> 6% of each run, Pallas kernels for 0% -> 0%
where the time goes in v1:
time: 237 us
  waiting for transfers between devices  113 us (48%)
  blocking collectives  52.5 us (22%)
  matrix products  27.1 us (11%)
  local copies, waits for them, and re-layouts  15.8 us (7%)
  between operations  13.5 us (6%)
  starting transfers between devices  9.21 us (4%)
  other arithmetic  5.74 us (2%)
    all_gather x1, waiting for transfers between devices, gathered_by_axis(): shard = lax.all_gather(shard, axis, axis=dim, tiled=True)  47 us
    all_to_all x1, waiting for transfers between devices, shards(): lax.all_to_all(jnp.stack([pair_elements] * lax.axis_size(GROW)), GROW, 0, 0)  40 us
    dot_general x3, matrix products, shards(): projected = jnp.dot(left_rows, kernel, preferred_element_type=jnp.float32)  27 us
    all_to_all x1, waiting for transfers between devices, turned_blocks(): out = lax.all_to_all(out, axes[k], k, k, tiled=True)  25.9 us
    all_to_all x1, blocking collectives, from_everyone(): return lax.all_to_all(copies, axis, split_axis=0, concat_axis=0, tiled=True)  19.4 us
    all_to_all x1, blocking collectives, summed_on_arrival(): lax.all_to_all(split_up(shard, dim, devices), axis, 0, 0, tiled=True)  15.2 us
    all_gather x1, blocking collectives, gathered_by_axis(): shard = lax.all_gather(shard, axis, axis=dim, tiled=True)  10.5 us
    all_to_all x1, blocking collectives, turned_blocks(): out = lax.all_to_all(out, axes[k], k, k, tiled=True)  7.26 us
  transfers between devices with their start and end apart: 3, of which 3 were waited for; matrix products, arithmetic and copies ran while one was open for 6% of the time, Pallas kernels for 0%

profile of v1, /device:TPU:1, one launch (start us, length us, event | category | flops | bytes accessed | tf_op | source)
XLA Modules:
  0.0 236.7 jit_solution(14691951150774784493)
XLA Ops:
  6.5 0.0 all-gather.2.cloned.1.call-start
  6.5 10.5 %all_gather.6 = bf16[2,64,1536]{2,1,0:T(8,128)(2,1)} all-gather(bf16[2,64,768]{2,1,0:T(8,128)(2,1)} %param.9), channel_id=1, replica_groups=mesh['grow_0'=2,'grow_1'=4,'grow_2'=2,'gcol_0'=8,'gcol_1'=2] {'gcol_1'}, dimensions={2}, use_global_device_ids=true | all-gather | bytes 589824 | tf_op jit(solution)/shard_map/all_gather | solution.py:14
  17.1 0.0 all-gather.2.cloned.1.call-update
  17.1 47.0 %all-gather.2.cloned.1.call-done = bf16[2,64,12288]{2,1,0:T(8,128)(2,1)} async-done(((bf16[2,64,1536]{2,1,0:T(8,128)(2,1)}), bf16[2,64,12288]{2,1,0:T(8,128)(2,1)}) %all-gather.2.cloned.1.call-update) | async-done | bytes 3145744 | tf_op jit(solution)/shard_map/all_gather | solution.py:14
  64.0 2.7 %copy.47 = bf16[16,8,16,768]{3,2,1,0:T(8,128)(2,1)S(1)} copy(bf16[16,8,16,768]{3,1,2,0:T(8,128)(2,1)} %bitcast.42) | data formatting | bytes 6291456
  66.7 0.2 bitcast_bitcast_fusion
  66.9 1.0 copy.36
  67.9 0.3 copy.37
  68.3 0.0 copy-start
  68.3 7.3 %all_to_all.25 = bf16[8,2,2,64,768]{4,3,2,0,1:T(8,128)(2,1)S(1)} all-to-all(bf16[8,2,2,64,768]{4,3,2,0,1:T(8,128)(2,1)S(1)} %copy.37), channel_id=1, replica_groups=mesh['grow_0'=2,'grow_1'=4,'grow_2'=2,'gcol_0'=8,'gcol_1'=2] {'grow_2'}, dimensions={1} | all-to-all | bytes 6291456 | tf_op jit(solution)/shard_map/all_to_all | solution.py:34
  75.5 0.0 copy-done
  75.5 2.1 stack.10
  77.6 5.6 %all-to-all-start.2 = ((bf16[16,2,64,768]{3,2,1,0:T(8,128)(2,1)}), bf16[16,2,64,768]{3,2,1,0:T(8,128)(2,1)}, u32[]{:S(2)}, u32[]{:S(2)}) async-start(bf16[16,2,64,768]{3,2,1,0:T(8,128)(2,1)} %stack.10), calls=%async_computation.2 | async-start | bytes 6291456 | tf_op jit(solution)/shard_map/all_to_all | solution.py:69
  83.2 1.9 copy.38
  85.1 0.0 copy-start.1
  85.1 0.0 copy-start.2
  85.1 40.0 %all-to-all-done.2 = bf16[16,2,64,768]{3,2,1,0:T(8,128)(2,1)} async-done(((bf16[16,2,64,768]{3,2,1,0:T(8,128)(2,1)}), bf16[16,2,64,768]{3,2,1,0:T(8,128)(2,1)}, u32[]{:S(2)}, u32[]{:S(2)}) %all-to-all-start.2) | async-done | bytes 3145760 | tf_op jit(solution)/shard_map/all_to_all | solution.py:69
  125.0 3.6 %all-to-all-start.1 = ((bf16[8,2,2,64,768]{4,3,2,1,0:T(8,128)(2,1)}), bf16[8,2,2,64,768]{4,3,2,1,0:T(8,128)(2,1)S(1)}, u32[]{:S(2)}, u32[]{:S(2)}) async-start(bf16[8,2,2,64,768]{4,3,2,1,0:T(8,128)(2,1)} %copy.38), calls=%async_computation.1 | async-start | bytes 6291456 | tf_op jit(solution)/shard_map/all_to_all | solution.py:34
  128.7 0.0 copy-done.1
  128.7 0.7 fusion.26
  129.4 0.0 copy-done.2
  129.4 0.1 divide_bitcast_fusion
  129.4 5.0 %bitcast_convert_fusion = f32[2048,768]{1,0:T(8,128)} fusion(bf16[16,2,64,768]{3,2,1,0:T(8,128)(2,1)} %all-to-all-done.2), kind=kLoop, calls=%fused_computation.12 | loop fusion | flops 1572864 | bytes 9437184 | tf_op jit(solution)/shard_map/convert_element_type | solution.py:88
  134.5 6.6 %copy.39 = f32[2048,768]{0,1:T(8,128)} copy(f32[2048,768]{1,0:T(8,128)} %bitcast_convert_fusion) | data formatting | bytes 12582912 | tf_op jit(solution)/shard_map/convert_element_type | solution.py:88
  141.1 25.9 %all-to-all-done.1 = bf16[8,2,2,64,768]{4,3,2,1,0:T(8,128)(2,1)S(1)} async-done(((bf16[8,2,2,64,768]{4,3,2,1,0:T(8,128)(2,1)}), bf16[8,2,2,64,768]{4,3,2,1,0:T(8,128)(2,1)S(1)}, u32[]{:S(2)}, u32[]{:S(2)}) %all-to-all-start.1) | async-done | bytes 3145760 | tf_op jit(solution)/shard_map/all_to_all | solution.py:34
  167.0 9.0 %fusion = bf16[2048]{0:T(1024)(128)(2,1)S(1)} fusion(f32[2048,768]{0,1:T(8,128)} %copy.39, bf16[2048,768]{1,0:T(8,128)(2,1)S(1)} %bitcast.39, f32[]{:T(128)} %bitcast.10, f32[768,768]{1,0:T(8,128)} %param.5, s32[768]{0:T(1024)S(1)} %get-tuple-element.8, s32[768]{0:T(1024)S(1)} %get-tuple-element.9, f32[768,768]{1,0:T(8,128)} %param.6), kind=kOutput, calls=%fused_computation.1 | convolution fusion | flops 2428499968 | bytes 14166020 | tf_op jit(solution)/shard_map/dot_general | solution.py:87
  176.0 0.1 stack.13
  176.1 9.0 %fusion.1 = bf16[2048]{0:T(1024)(128)(2,1)S(1)} fusion(f32[2048,768]{0,1:T(8,128)} %copy.39, bf16[2048,768]{1,0:T(8,128)(2,1)S(1)} %bitcast.40, f32[]{:T(128)} %bitcast.7, f32[768,768]{1,0:T(8,128)} %param.5, s32[768]{0:T(1024)S(1)} %get-tuple-element.8, s32[768]{0:T(1024)S(1)} %get-tuple-element.9, f32[768,768]{1,0:T(8,128)} %param.6), kind=kOutput, calls=%fused_computation.3 | convolution fusion | flops 2428499968 | bytes 14166020 | tf_op jit(solution)/shard_map/dot_general | solution.py:87
  185.1 0.1 stack.12
  185.1 9.0 %fusion.2 = bf16[2048]{0:T(1024)(128)(2,1)S(1)} fusion(f32[2048,768]{0,1:T(8,128)} %copy.39, bf16[2048,768]{1,0:T(8,128)(2,1)S(1)} %bitcast.41, f32[]{:T(128)} %bitcast.1, f32[768,768]{1,0:T(8,128)} %param.5, s32[768]{0:T(1024)S(1)} %get-tuple-element.8, s32[768]{0:T(1024)S(1)} %get-tuple-element.9, f32[768,768]{1,0:T(8,128)} %param.6), kind=kOutput, calls=%fused_computation.5 | convolution fusion | flops 2428499968 | bytes 14166020 | tf_op jit(solution)/shard_map/dot_general | solution.py:87
  194.2 0.1 stack.11
  194.2 0.1 fusion.18
  194.4 0.1 reshape.32
  194.5 15.2 %all_to_all.26 = f32[16,3,4]{2,1,0:T(4,128)S(1)} all-to-all(f32[16,3,4]{2,1,0:T(4,128)S(1)} %copy.42), channel_id=1, replica_groups=mesh['grow_0'=2,'grow_1'=4,'grow_2'=2,'gcol_0'=8,'gcol_1'=2] {'gcol_0','..., dimensions={0} | all-to-all | bytes 1536 | tf_op jit(solution)/shard_map/all_to_all | solution.py:46
  209.8 19.4 %all_to_all.27 = f32[16,3,4]{2,1,0:T(4,128)S(1)} all-to-all(f32[16,3,4]{2,1,0:T(4,128)S(1)} %broadcast_in_dim.2), channel_id=1, replica_groups=mesh['grow_0'=2,'grow_1'=4,'grow_2'=2,'gcol_0'=8,'gcol_1'=2] {'grow_0','..., dimensions={0} | all-to-all | bytes 1536 | tf_op jit(solution)/shard_map/all_to_all | solution.py:52
  229.2 0.6 reduce_sum.49
  (5 shorter events, 0.1 us)
Async XLA Ops:
  6.5 57.5 %all-gather.2.cloned.1.call-start = ((), (), s32[]{:S(2)}) async-start(), calls=%async_computation.5 | async-start | bytes 3538944 | tf_op jit(solution)/shard_map/all_gather | solution.py:14
  68.3 7.3 %copy-start = (bf16[2,64,768]{2,1,0:T(8,128)(2,1)S(1)}, bf16[2,64,768]{2,1,0:T(8,128)(2,1)}, u32[]{:S(2)}) copy-start(bf16[2,64,768]{2,1,0:T(8,128)(2,1)} %param.9) | copy-start | bytes 589828
  77.6 47.4 %all-to-all-start.2 = ((bf16[16,2,64,768]{3,2,1,0:T(8,128)(2,1)}), bf16[16,2,64,768]{3,2,1,0:T(8,128)(2,1)}, u32[]{:S(2)}, u32[]{:S(2)}) async-start(bf16[16,2,64,768]{3,2,1,0:T(8,128)(2,1)} %stack.10), calls=%async_computation.2 | async-start | bytes 6291456 | tf_op jit(solution)/shard_map/all_to_all | solution.py:69
  85.1 43.7 %copy-start.1 = (f32[3]{0:T(128)S(1)}, f32[3]{0:T(128)}, u32[]{:S(2)}) copy-start(f32[3]{0:T(128)} %param.7) | copy-start | bytes 40
  85.1 44.3 %copy-start.2 = (f32[32]{0:T(128)S(1)}, f32[32]{0:T(128)}, u32[]{:S(2)}) copy-start(f32[32]{0:T(128)} %param.8) | copy-start | bytes 388
  125.0 41.9 %all-to-all-start.1 = ((bf16[8,2,2,64,768]{4,3,2,1,0:T(8,128)(2,1)}), bf16[8,2,2,64,768]{4,3,2,1,0:T(8,128)(2,1)S(1)}, u32[]{:S(2)}, u32[]{:S(2)}) async-start(bf16[8,2,2,64,768]{4,3,2,1,0:T(8,128)(2,1)} %copy.38), calls=%async_computation.1 | async-start | bytes 6291456 | tf_op jit(solution)/shard_map/all_to_all | solution.py:34
Sparse Core Ops, SparseCore 0:
  17.2 46.8 all-gather.1
